TPU v7x, 32 devices: a whole 2x2x4 slice. The times are simulated.
32 devices in a mesh: grp: 4 (over z), wave: 8 (over y, x, core).
Axes of the slice: x: 2, y: 2, z: 4, core: 2. Of those that a mesh axis runs over, the one named last changes fastest.
Arguments:
- state: bfloat16 [275, 61760], P(None, ('grp', 'wave')), may hold values from -6 to 6
- held_orders: int32 [160], P(('grp', 'wave')), may hold values from -1 to 95, as said below
- pair_lows: int32 [96], P(('grp', 'wave')), may hold values from 0 to 95, each once
- inverses: bfloat16 [96, 2, 137, 137], P(('grp', 'wave')), may hold values from -2 to 3
- height_operator: bfloat16 [137, 137], replicated, may hold values from -0.5 to 0.5
- pressure_column: bfloat16 [137], replicated, may hold values from -5 to 5
- thermal_response_matrix: bfloat16 [137, 137], replicated, may hold values from -0.5 to 0.5
- mass_row: bfloat16 [137], replicated, may hold values from -0.5 to 0.5
Outputs:
- advanced: bfloat16 [275, 61760], P(None, ('grp', 'wave'))
Inputs may be any that keep to these rules, and one draw needn't show every extreme that they name: `held_orders`: each of 0 to 95 appears exactly once, all other entries are -1; some device has all 5 of its slots filled.
All inputs are finite; a program needn't handle non-finite values.
Results may differ from a plain program's by a relative error of at most 0.0052.
Values may be sent and summed in bfloat16 or wider, within the bound.
A program may use at most 128 MiB of HBM per device.

v0:
```python
import jax
import jax.numpy as jnp
from jax import lax
from jax.sharding import PartitionSpec as P


def send_out(message):
    return lax.all_to_all(message, ("grp", "wave"), split_axis=1, concat_axis=1, tiled=True)


def send_home(message):
    return lax.all_to_all(message, ("grp", "wave"), split_axis=1, concat_axis=1, tiled=True)


def solve_columns(inverses, right_side):
    shape = right_side.shape
    shaped = right_side.reshape(shape[0], shape[1], shape[2], 3, -1)
    matrices = jnp.stack([inverses[:, 0], inverses[:, 1], inverses[:, 1]], axis=1)
    solved = jnp.einsum("jtkl,lajtc->kajtc", matrices, shaped, preferred_element_type=jnp.float32)
    return solved.astype(jnp.bfloat16).reshape(shape)


def shards(
    state,
    held_orders,
    pair_lows,
    inverses,
    height_operator,
    pressure_column,
    thermal_response_matrix,
    mass_row,
):
    layer_heights_count = height_operator.shape[0]
    pair_count = pair_lows.shape[0]
    slot_count = held_orders.shape[0]
    devices = lax.axis_size("grp") * lax.axis_size("wave")
    truncation = 2 * pair_count * devices - 1
    slot_width = 2 * (truncation + 2)
    denom = float(truncation * (truncation + 1))
    fill_col = slot_count * slot_width
    all_lows = lax.all_gather(pair_lows, ("grp", "wave"), axis=0, tiled=True)
    low_table = all_lows.reshape(devices, pair_count, 1, 1, 1)
    orders = held_orders.reshape(1, 1, 1, slot_count, 1)
    member = jnp.arange(3, dtype=jnp.int32).reshape(1, 1, 3, 1, 1)
    halves = jnp.arange(2, dtype=jnp.int32).reshape(1, 1, 1, 1, 2)
    slot_ids = jnp.arange(slot_count, dtype=jnp.int32).reshape(1, 1, 1, slot_count, 1)
    position = jnp.where(
        member == 0,
        low_table - orders,
        jnp.where(member == 1, truncation - low_table - orders, truncation + 1 - low_table),
    )
    usable = (orders >= 0) & jnp.where(
        member == 0, orders <= low_table, jnp.where(member == 1, True, orders >= low_table)
    )
    column = slot_ids * slot_width + 2 * position + halves
    column = jnp.where(usable, column, fill_col).reshape(-1)
    low_mask = jnp.broadcast_to(member == 0, (devices, pair_count, 3, slot_count, 2)).reshape(
        devices, pair_count, -1
    )
    per_pair = low_mask.shape[2]
    recv_shape = (devices, pair_count, per_pair)
    divergence = state[:layer_heights_count]
    thermal_state_array = state[layer_heights_count : 2 * layer_heights_count]
    pressure = state[2 * layer_heights_count]
    coeff_index = (jnp.arange(slot_width, dtype=jnp.int32) // 2)[None, :]
    order_col = held_orders[:, None]
    degree = jnp.where(
        coeff_index <= truncation - order_col, order_col + coeff_index, coeff_index - 1
    )
    lap_scale = ((degree * (degree + 1)).astype(jnp.float32) / denom).reshape(-1)
    height_drive_term = jnp.dot(
        height_operator, thermal_state_array, preferred_element_type=jnp.float32
    )
    height_drive_term = (
        height_drive_term
        + pressure_column.astype(jnp.float32)[:, None] * pressure.astype(jnp.float32)[None, :]
    )
    right_side = (divergence.astype(jnp.float32) + lap_scale[None, :] * height_drive_term).astype(
        jnp.bfloat16
    )
    message = jnp.take(right_side, column, axis=1, mode="fill", fill_value=0)
    arriving_arrays = send_out(message).reshape((layer_heights_count,) + recv_shape)
    div_sent = solve_columns(inverses, arriving_arrays).reshape(layer_heights_count, -1)
    returned = send_home(div_sent)
    next_spreading_rate = (
        jnp.zeros((layer_heights_count, fill_col), jnp.bfloat16)
        .at[:, column]
        .set(returned, mode="drop")
    )
    next_thermal_state = (
        thermal_state_array.astype(jnp.float32)
        - jnp.dot(thermal_response_matrix, next_spreading_rate, preferred_element_type=jnp.float32)
    ).astype(jnp.bfloat16)
    surface_mass_next = (
        pressure.astype(jnp.float32)
        - jnp.dot(mass_row, next_spreading_rate, preferred_element_type=jnp.float32)
    ).astype(jnp.bfloat16)
    live_slot = jnp.repeat(held_orders >= 0, slot_width)[None, :]
    result = jnp.concatenate(
        [next_spreading_rate, next_thermal_state, surface_mass_next[None, :]], axis=0
    )
    return jnp.where(live_slot, result, jnp.zeros_like(result))


def solution(mesh):
    placed = (
        P(None, ("grp", "wave")),
        P(("grp", "wave")),
        P(("grp", "wave")),
        P(("grp", "wave"), None, None, None),
        P(),
        P(),
        P(),
        P(),
    )
    return jax.shard_map(
        shards, mesh=mesh, in_specs=placed, out_specs=P(None, ("grp", "wave")), check_vma=False
    )
```

profile of v0, /device:TPU:0, one launch (start us, length us, event | category | flops | bytes accessed | tf_op | source)
XLA Modules:
  0.0 162.0 jit_solution(7955989957492529605)
XLA Ops:
  0.0 0.9 dynamic-update-slice
  0.9 42.0 %all-reduce = s32[96]{0:T(128)S(1)} all-reduce(s32[96]{0:T(128)S(1)} %dynamic-update-slice), channel_id=1, replica_groups=mesh['grp'=4,'wave'=8] {'grp','wave'}, use_global_device_ids=true, to_apply=%add | all-reduce | flops 96 | bytes 768
  44.5 0.7 broadcast_compare_fusion.1
  45.2 0.7 broadcast_subtract_fusion.3
  47.3 0.8 slice_convert_fusion
  48.1 1.6 %fusion.3 = bf16[137,1930]{1,0:T(8,128)(2,1)S(1)} fusion(bf16[137,137]{1,0:T(8,128)(2,1)S(1)} %copy-done, f32[1930]{0:T(1024)S(1)} %bitcast.32, f32[137]{0:T(256)S(1)} %convert_element_type.37, f32[1930]{0:T(1024)S(1)} %fusion.12, bf16[275,1930]{1,0:T(8,128)(2,1)} %param.8), kind=kOutput, calls=%fused_computation.7 | convolution fusion | flops 74034784 | bytes 1761994 | tf_op jit(solution)/shard_map/dot_general | solution.py:71
  49.8 0.8 copy.36
  50.6 9.2 %gather_fusion = bf16[2880,137]{1,0:T(8,128)(2,1)S(1)} fusion(bf16[137,1930]{0,1:T(8,128)(2,1)S(1)} %copy.36, s32[3072]{0:T(1024)S(1)} %pad_clamp_fusion), kind=kCustom, calls=%fused_computation | custom fusion | bytes 1589760 | tf_op jit(solution)/shard_map/jit(_take)/gather | solution.py:81
  59.8 1.0 copy.37
  60.7 4.0 %gather.7 = bf16[137,32,90]{2,1,0:T(8,128)(2,1)S(1)} reshape(bf16[137,2880]{1,0:T(8,128)(2,1)S(1)} %copy.37) | data formatting | bytes 1578240 | tf_op jit(solution)/shard_map/jit(_take)/gather | solution.py:81
  65.0 1.5 copy.38
  66.4 4.4 %all-to-all-start = ((bf16[137,32,90]{2,0,1:T(8,128)(2,1)}), bf16[137,32,90]{2,0,1:T(8,128)(2,1)S(1)}, u32[]{:S(2)}, u32[]{:S(2)}) async-start(bf16[137,32,90]{2,0,1:T(8,128)(2,1)} %copy.38), calls=%async_computation | async-start | bytes 2359296 | tf_op jit(solution)/shard_map/all_to_all | solution.py:8
  71.6 28.2 %all-to-all-done = bf16[137,32,90]{2,0,1:T(8,128)(2,1)S(1)} async-done(((bf16[137,32,90]{2,0,1:T(8,128)(2,1)}), bf16[137,32,90]{2,0,1:T(8,128)(2,1)S(1)}, u32[]{:S(2)}, u32[]{:S(2)}) %all-to-all-start) | async-done | bytes 789152 | tf_op jit(solution)/shard_map/all_to_all | solution.py:8
  99.9 2.3 %copy.39 = bf16[137,32,90]{0,1,2:T(8,128)(2,1)S(1)} copy(bf16[137,32,90]{2,0,1:T(8,128)(2,1)S(1)} %all-to-all-done) | data formatting | bytes 1578240 | tf_op jit(solution)/shard_map/all_to_all | solution.py:8
  102.2 1.5 convolution_convert_fusion
  103.7 2.5 %copy.42 = bf16[137,32,90]{2,0,1:T(8,128)(2,1)} copy(bf16[137,32,90]{0,1,2:T(8,128)(2,1)S(1)} %bitcast.28) | data formatting | bytes 1578240 | tf_op jit(solution)/shard_map/all_to_all | solution.py:12
  106.2 3.8 %all-to-all-start.1 = ((bf16[137,32,90]{2,0,1:T(8,128)(2,1)}), bf16[137,32,90]{2,0,1:T(8,128)(2,1)S(1)}, u32[]{:S(2)}, u32[]{:S(2)}) async-start(bf16[137,32,90]{2,0,1:T(8,128)(2,1)} %copy.42), calls=%async_computation.1 | async-start | bytes 2359296 | tf_op jit(solution)/shard_map/all_to_all | solution.py:12
  110.2 28.6 %all-to-all-done.1 = bf16[137,32,90]{2,0,1:T(8,128)(2,1)S(1)} async-done(((bf16[137,32,90]{2,0,1:T(8,128)(2,1)}), bf16[137,32,90]{2,0,1:T(8,128)(2,1)S(1)}, u32[]{:S(2)}, u32[]{:S(2)}) %all-to-all-start.1) | async-done | bytes 789152 | tf_op jit(solution)/shard_map/all_to_all | solution.py:12
  139.1 2.4 %reshape.228 = bf16[137,2880]{1,0:T(8,128)(2,1)S(1)} reshape(bf16[137,32,90]{2,1,0:T(8,128)(2,1)S(1)} %copy.43) | data formatting | bytes 1578240 | tf_op jit(solution)/shard_map/all_to_all | solution.py:12
  141.5 1.0 copy.44
  142.6 15.4 %scatter_custom_fusion = bf16[137,1930]{0,1:T(8,128)(2,1)S(1)} fusion(s32[2880]{0:T(1024)S(1)} %fusion.10, bf16[2880,137]{1,0:T(8,128)(2,1)S(1)} %copy.44, bf16[]{:T(256)} %constant.23.clone.1), kind=kCustom, calls=%fused_computation.16 | custom fusion | bytes 528822 | tf_op jit(solution)/shard_map/scatter | solution.py:88
  158.0 0.7 copy.45
  158.7 1.5 fusion.4
  160.7 1.3 maximum_select_fusion
  (47 shorter events, 4.7 us)
Async XLA Ops:
  0.0 48.1 %copy-start = (bf16[137,137]{1,0:T(8,128)(2,1)S(1)}, bf16[137,137]{1,0:T(8,128)(2,1)}, u32[]{:S(2)}) copy-start(bf16[137,137]{1,0:T(8,128)(2,1)} %param.12) | copy-start | bytes 112618
  46.2 0.9 copy-start.2
  46.2 1.9 %copy-start.4 = (bf16[137]{0:T(256)(128)(2,1)S(1)}, bf16[137]{0:T(256)(128)(2,1)}, u32[]{:S(2)}) copy-start(bf16[137]{0:T(256)(128)(2,1)} %param.13) | copy-start | bytes 826
  66.4 4.4 %copy-start.1 = (bf16[3,2,137,137]{3,1,2,0:T(2,128)(2,1)S(1)}, bf16[3,2,137,137]{3,1,2,0:T(2,128)(2,1)}, u32[]{:S(2)}) copy-start(bf16[3,2,137,137]{3,1,2,0:T(2,128)(2,1)} %param.11) | copy-start | bytes 675688
  66.4 33.4 %all-to-all-start = ((bf16[137,32,90]{2,0,1:T(8,128)(2,1)}), bf16[137,32,90]{2,0,1:T(8,128)(2,1)S(1)}, u32[]{:S(2)}, u32[]{:S(2)}) async-start(bf16[137,32,90]{2,0,1:T(8,128)(2,1)} %copy.38), calls=%async_computation | async-start | bytes 2359296 | tf_op jit(solution)/shard_map/all_to_all | solution.py:8
  106.2 3.8 %copy-start.5 = (bf16[137]{0:T(256)(128)(2,1)S(1)}, bf16[137]{0:T(256)(128)(2,1)}, u32[]{:S(2)}) copy-start(bf16[137]{0:T(256)(128)(2,1)} %param.15) | copy-start | bytes 826
  106.2 32.6 %all-to-all-start.1 = ((bf16[137,32,90]{2,0,1:T(8,128)(2,1)}), bf16[137,32,90]{2,0,1:T(8,128)(2,1)S(1)}, u32[]{:S(2)}, u32[]{:S(2)}) async-start(bf16[137,32,90]{2,0,1:T(8,128)(2,1)} %copy.42), calls=%async_computation.1 | async-start | bytes 2359296 | tf_op jit(solution)/shard_map/all_to_all | solution.py:12
  142.6 16.2 %copy-start.3 = (bf16[137,137]{1,0:T(8,128)(2,1)S(1)}, bf16[137,137]{1,0:T(8,128)(2,1)}, u32[]{:S(2)}) copy-start(bf16[137,137]{1,0:T(8,128)(2,1)} %param.14) | copy-start | bytes 112618
where the time goes:
time: 163 us; the launch traced here: 162 us
  waiting for transfers between devices  56.9 us (35%)
  local copies, waits for them, and re-layouts  44.3 us (27%)
  blocking collectives  42 us (26%)
  starting transfers between devices  8.2 us (5%)
  other arithmetic  5.33 us (3%)
  matrix products  5.05 us (3%)
    unnamed x1, blocking collectives  42 us
    all_to_all x1, waiting for transfers between devices, send_home(): lax.all_to_all(message, ('grp', 'wave'), split_axis=1, concat_axis=1, til...  28.6 us
    all_to_all x1, waiting for transfers between devices, send_out(): lax.all_to_all(message, ('grp', 'wave'), split_axis=1, concat_axis=1, til...  28.2 us
    scatter x2, local copies, waits for them, and re-layouts, shards(): next_spreading_rate = jnp.zeros((layer_heights_count, fill_col), jnp.bflo...  16.1 us
    gather x3, local copies, waits for them, and re-layouts, shards(): message = jnp.take(right_side, column, axis=1, mode='fill', fill_value=0)  14.1 us
    all_to_all x4, local copies, waits for them, and re-layouts, send_home(): lax.all_to_all(message, ('grp', 'wave'), split_axis=1, concat_axis=1, til...  6.22 us
    all_to_all x1, starting transfers between devices, send_out(): lax.all_to_all(message, ('grp', 'wave'), split_axis=1, concat_axis=1, til...  4.4 us
    all_to_all x1, starting transfers between devices, send_home(): lax.all_to_all(message, ('grp', 'wave'), split_axis=1, concat_axis=1, til...  3.8 us
  transfers between devices with their start and end apart: 2, of which 2 were waited for; matrix products, arithmetic and copies ran while one was open for 1% of the time, Pallas kernels for 0%

commit v1 on v0

v1 whole, which is shorter than its diff:
```python
import functools

import jax
import jax.numpy as jnp
from jax import lax
from jax.experimental import pallas as pl
from jax.experimental.pallas import tpu as pltpu
from jax.sharding import PartitionSpec as P

MESH = pl.DeviceIdType.MESH
LANES = 128
ROWS_TILE = 16
KEEP_BYTES = 24 << 20


def ceil_to(value, step):
    return -(-value // step) * step


def kernel(
    size,
    held,
    lows,
    state,
    inverses,
    height,
    response,
    out,
    info,
    matrices,
    rest,
    right,
    pick,
    outgoing,
    arrived,
    solved,
    returned,
    total,
    info_send,
    info_recv,
    z_send,
    z_recv,
    out_send,
    out_recv,
    back_send,
    back_recv,
):
    Z, W, levels, slots, pairs = size
    half_count = Z * W * pairs
    truncation = 2 * half_count - 1
    slot_width = 2 * (truncation + 2)
    width = slots * slot_width
    denom = float(truncation * (truncation + 1))
    devices = Z * W
    per_pair = 4 * slots
    block_pairs = Z * pairs // 2
    first_extra = block_pairs * per_pair
    tail = levels - LANES
    chunks = pairs + 1
    keep = pick.shape[0] > 1
    z = lax.axis_index("grp")
    w = lax.axis_index("wave")
    me = z * W + w

    barrier = pltpu.get_barrier_semaphore()

    def greet(k, carry):
        other = lax.rem(me + k, devices)
        pl.semaphore_signal(
            barrier, inc=1, device_id=(other // W, lax.rem(other, W)), device_id_type=MESH
        )
        return carry

    lax.fori_loop(1, devices, greet, 0)

    lane = lax.broadcasted_iota(jnp.int32, (1, LANES), 1)
    extra = lane >= first_extra
    used = lane < first_extra + slots
    lane_pair = lane // per_pair
    lane_member = lax.rem(lane, per_pair) // (2 * slots)
    lane_slot = jnp.where(extra, lane - first_extra, lax.rem(lane, 2 * slots) // 2)
    orders = jnp.full((1, LANES), -1, jnp.int32)
    for s in range(slots):
        orders = jnp.where(lane_slot == s, held[s], orders)
    row = lax.broadcasted_iota(jnp.int32, (pairs + 1, LANES), 0)
    tile = jnp.broadcast_to(orders, (pairs + 1, LANES))
    for j in range(pairs):
        tile = jnp.where(row == j, lows[j], tile)
    info[me] = tile

    ends = []
    for i in range(2 * pairs):
        matrices[z, i, 0:levels, :] = inverses[i]
        ends.append(inverses[i, :, LANES:levels].astype(jnp.float32))
    ends = jnp.concatenate(ends, axis=1).astype(jnp.bfloat16)
    rest[z, 0:levels, 0 : 2 * pairs * tail] = ends

    pl.semaphore_wait(barrier, devices - 1)

    def info_copy(k):
        other = lax.rem(me + k, devices)
        return pltpu.make_async_remote_copy(
            src_ref=info.at[me],
            dst_ref=info.at[me],
            send_sem=info_send.at[k],
            recv_sem=info_recv.at[k],
            device_id=(other // W, lax.rem(other, W)),
            device_id_type=MESH,
        )

    def info_arrival(k):
        source = lax.rem(me + devices - k, devices)
        return pltpu.make_async_remote_copy(
            src_ref=info.at[source],
            dst_ref=info.at[source],
            send_sem=info_send.at[k],
            recv_sem=info_recv.at[k],
            device_id=(source // W, lax.rem(source, W)),
            device_id_type=MESH,
        )

    def start_info(k, carry):
        info_copy(k).start()
        return carry

    lax.fori_loop(1, devices, start_info, 0)

    def z_copy(g, c, way):
        if c < pairs:
            ref = matrices.at[g, pl.ds(2 * c, 2), :, pl.ds(0, LANES)]
        else:
            ref = rest.at[g]
        step = 1 if way == 0 else -1
        return pltpu.make_async_remote_copy(
            src_ref=ref,
            dst_ref=ref,
            send_sem=z_send.at[g, c, way],
            recv_sem=z_recv.at[g, c],
            device_id=(z + step, w),
            device_id_type=MESH,
        )

    def forward(g, c):
        @pl.when(jnp.logical_and(g <= z, z < Z - 1))
        def _():
            z_copy(g, c, 0).start()

        @pl.when(jnp.logical_and(g >= z, z > 0))
        def _():
            z_copy(g, c, 1).start()

    def group_at(t):
        g = z
        for zz in range(Z):
            by_distance = sorted(range(Z), key=lambda a: abs(a - zz))
            g = jnp.where(z == zz, by_distance[t], g)
        return g

    def relay(t):
        g = group_at(t)
        for c in range(chunks):
            z_copy(g, c, 0).wait_recv()
            forward(g, c)

    for c in range(chunks):
        forward(z, c)

    column = lax.broadcasted_iota(jnp.int32, (1, width), 1)
    column_order = jnp.full((1, width), -1, jnp.int32)
    column_start = jnp.zeros((1, width), jnp.int32)
    for s in range(slots):
        inside = jnp.logical_and(column >= s * slot_width, column < (s + 1) * slot_width)
        column_order = jnp.where(inside, held[s], column_order)
        column_start = jnp.where(inside, s * slot_width, column_start)
    coefficient = (column - column_start) // 2
    degree = jnp.where(
        coefficient <= truncation - column_order, column_order + coefficient, coefficient - 1
    )
    lap_scale = (degree * (degree + 1)).astype(jnp.float32) / denom
    drive = jnp.dot(height[...], state[LANES:, :], preferred_element_type=jnp.float32)
    right[0:levels, :] = (
        state[0:levels, :].astype(jnp.float32) + lap_scale * drive
    ).astype(jnp.bfloat16)

    def wait_info(k, carry):
        info_arrival(k).wait_recv()
        return carry

    lax.fori_loop(1, devices, wait_info, 0)

    def build(k, place):
        d = lax.rem(w + k, W)
        tables = [info[g * W + d] for g in range(Z)]
        low_rows = [tables[g][j : j + 1] for g in range(Z) for j in range(pairs)]
        hit = low_rows[0] == orders
        for low in low_rows[1:]:
            hit = jnp.logical_or(hit, low == orders)
        for b in range(2):
            low = jnp.zeros((1, LANES), jnp.int32)
            for p in range(block_pairs):
                low = jnp.where(lane_pair == p, low_rows[b * block_pairs + p], low)
            merged = jnp.where(orders <= low, low - orders, truncation + 1 - low)
            position = jnp.where(lane_member == 0, merged, truncation - low - orders)
            position = jnp.where(extra, truncation + 1 - orders, position)
            part = jnp.where(extra, b, lax.rem(lane, 2))
            target = lane_slot * slot_width + 2 * position + part
            target = jnp.where(jnp.logical_and(orders >= 0, used), target, -1)
            target = jnp.where(jnp.logical_and(extra, jnp.logical_not(hit)), -1, target)
            at = lax.broadcasted_iota(jnp.int32, (width, LANES), 0)
            pick[place, :, b * LANES : (b + 1) * LANES] = jnp.where(
                at == target, 1.0, 0.0
            ).astype(jnp.bfloat16)

    def place_of(k):
        return k if keep else 0

    def out_copy(k):
        return pltpu.make_async_remote_copy(
            src_ref=outgoing.at[k],
            dst_ref=arrived.at[k],
            send_sem=out_send.at[k],
            recv_sem=out_recv.at[k],
            device_id=(z, lax.rem(w + k, W)),
            device_id_type=MESH,
        )

    def back_copy(k):
        return pltpu.make_async_remote_copy(
            src_ref=solved.at[k],
            dst_ref=returned.at[k],
            send_sem=back_send.at[k],
            recv_sem=back_recv.at[k],
            device_id=(z, lax.rem(w + W - k, W)),
            device_id_type=MESH,
        )

    def message(k):
        build(k, place_of(k))
        return jnp.dot(
            right[...], pick[place_of(k)], preferred_element_type=jnp.float32
        ).astype(jnp.bfloat16)

    def send(k, carry):
        outgoing[k] = message(k)
        out_copy(k).start()
        return carry

    middle = W // 2 + 1
    lax.fori_loop(1, middle, send, 0)
    relay(1)
    lax.fori_loop(middle, W, send, 0)
    arrived[0] = message(0)

    for t in range(2, Z - 1):
        relay(t)

    def wait_out(k, carry):
        out_copy(k).wait_recv()
        return carry

    lax.fori_loop(1, W, wait_out, 0)

    wide_lane = jnp.concatenate([lane, lane], axis=1)
    wide_pair = wide_lane // per_pair
    wide_member = lax.rem(wide_lane, per_pair) // (2 * slots)
    wide_extra = jnp.logical_and(wide_lane >= first_extra, wide_lane < first_extra + slots)

    def solve(t):
        g = group_at(t)
        b = (g * pairs) // block_pairs
        for i in range(2 * pairs):
            if t > 0:
                piece = rest[g].astype(jnp.float32)[:, i * tail : (i + 1) * tail]
                matrices[g, i, :, LANES:levels] = piece.astype(jnp.bfloat16)
        near = pl.ds(pl.multiple_of(b * LANES, LANES), LANES)
        far = pl.ds(pl.multiple_of((1 - b) * LANES, LANES), LANES)
        mine = info[g * W + w]

        def two_sources(i, carry):
            k0, k1 = 2 * i, 2 * i + 1
            s0 = lax.rem(w + W - k0, W)
            s1 = lax.rem(w + W - k1, W)
            m0 = info[z * W + s0][pairs : pairs + 1]
            m1 = info[z * W + s1][pairs : pairs + 1]
            m = jnp.concatenate([m0, m1], axis=1)
            x_near = jnp.concatenate(
                [arrived[k0, 0:levels, near], arrived[k1, 0:levels, near]], axis=1
            )
            x_far = jnp.concatenate(
                [arrived[k0, 0:levels, far], arrived[k1, 0:levels, far]], axis=1
            )
            if t == 0:
                y_near = jnp.zeros((solved.shape[1], 2 * LANES), jnp.float32)
                y_far = y_near
            else:
                y_near = jnp.concatenate([solved[k0, :, near], solved[k1, :, near]], axis=1)
                y_far = jnp.concatenate([solved[k0, :, far], solved[k1, :, far]], axis=1)
                y_near = y_near.astype(jnp.float32)
                y_far = y_far.astype(jnp.float32)
            for j in range(pairs):
                low = jnp.concatenate([mine[j : j + 1]] * 2, axis=1)
                here = g * pairs + j - b * block_pairs
                own = wide_pair == here
                use_extra = jnp.logical_and(wide_extra, m == low)
                use_low = jnp.logical_and(jnp.logical_and(own, wide_member == 0), m <= low)
                use_high = jnp.logical_or(own, use_extra)
                lower = jnp.dot(matrices[g, 2 * j], x_near, preferred_element_type=jnp.float32)
                upper = jnp.dot(matrices[g, 2 * j + 1], x_near, preferred_element_type=jnp.float32)
                upper_far = jnp.dot(
                    matrices[g, 2 * j + 1], x_far, preferred_element_type=jnp.float32
                )
                y_near = jnp.where(use_low, lower, jnp.where(use_high, upper, y_near))
                y_far = jnp.where(use_extra, upper_far, y_far)
            y_near = y_near.astype(jnp.bfloat16)
            y_far = y_far.astype(jnp.bfloat16)
            solved[k0, :, near] = y_near[:, :LANES]
            solved[k1, :, near] = y_near[:, LANES:]
            solved[k0, :, far] = y_far[:, :LANES]
            solved[k1, :, far] = y_far[:, LANES:]
            if t == Z - 1:

                @pl.when(i > 0)
                def _():
                    back_copy(k0).start()

                back_copy(k1).start()
            return carry

        lax.fori_loop(0, W // 2, two_sources, 0)

    for t in range(Z):
        if t == Z - 1:
            relay(t)
        solve(t)

    total[...] = jnp.zeros_like(total)

    def collect(k, block):
        if not keep:
            build(k, 0)
        total[...] += lax.dot_general(
            block, pick[place_of(k)], (((1,), (1,)), ((), ())), preferred_element_type=jnp.float32
        )

    collect(0, solved[0])

    def gather_back(k, carry):
        back_copy(k).wait_recv()
        collect(k, returned[k])
        return carry

    lax.fori_loop(1, W, gather_back, 0)

    div = total[0:levels, :].astype(jnp.bfloat16)
    change = jnp.dot(response[...], div, preferred_element_type=jnp.float32)
    old = state[LANES:, :].astype(jnp.float32)
    below = lax.broadcasted_iota(jnp.int32, old.shape, 0) < tail
    new = jnp.where(below, 0.0, old) - change
    new = jnp.where(column_order >= 0, new, 0.0)
    out[0:LANES, :] = div[0:LANES, :]
    out[LANES:, :] = new.astype(jnp.bfloat16)

    def drain(k, carry):
        out_copy(k).wait_send()
        back_copy(k).wait_send()
        return carry

    lax.fori_loop(1, W, drain, 0)

    def drain_info(k, carry):
        info_copy(k).wait_send()
        return carry

    lax.fori_loop(1, devices, drain_info, 0)
    for g in range(Z):
        for c in range(chunks):

            @pl.when(jnp.logical_and(g <= z, z < Z - 1))
            def _():
                z_copy(g, c, 0).wait_send()

            @pl.when(jnp.logical_and(g >= z, z > 0))
            def _():
                z_copy(g, c, 1).wait_send()


def shards(
    state,
    held_orders,
    pair_lows,
    inverses,
    height_operator,
    pressure_column,
    thermal_response_matrix,
    mass_row,
):
    levels = height_operator.shape[0]
    slots = held_orders.shape[0]
    pairs = pair_lows.shape[0]
    Z, W = lax.axis_size("grp"), lax.axis_size("wave")
    devices = Z * W
    width = state.shape[1]
    tail = levels - LANES
    rows = ceil_to(levels, ROWS_TILE)
    height = jnp.concatenate(
        [jnp.zeros((levels, tail), jnp.bfloat16), height_operator, pressure_column[:, None]], axis=1
    )
    through = -jnp.eye(tail, levels, LANES, dtype=jnp.bfloat16)
    response = jnp.concatenate([through, thermal_response_matrix, mass_row[None, :]], axis=0)
    places = W if W * width * 4 * LANES <= KEEP_BYTES else 1
    vmem = pl.BlockSpec(memory_space=pltpu.VMEM)
    smem = pl.BlockSpec(memory_space=pltpu.SMEM)
    block = pltpu.VMEM((W, rows, 2 * LANES), jnp.bfloat16)
    return pl.pallas_call(
        functools.partial(kernel, (Z, W, levels, slots, pairs)),
        out_shape=jax.ShapeDtypeStruct(state.shape, jnp.bfloat16),
        in_specs=[smem, smem, vmem, vmem, vmem, vmem],
        out_specs=vmem,
        scratch_shapes=[
            pltpu.VMEM((devices, pairs + 1, LANES), jnp.int32),
            pltpu.VMEM((Z, 2 * pairs, rows, levels), jnp.bfloat16),
            pltpu.VMEM((Z, rows, LANES), jnp.bfloat16),
            pltpu.VMEM((rows, width), jnp.bfloat16),
            pltpu.VMEM((places, width, 2 * LANES), jnp.bfloat16),
            block,
            block,
            block,
            block,
            pltpu.VMEM((rows, width), jnp.float32),
            pltpu.SemaphoreType.DMA((devices,)),
            pltpu.SemaphoreType.DMA((devices,)),
            pltpu.SemaphoreType.DMA((Z, pairs + 1, 2)),
            pltpu.SemaphoreType.DMA((Z, pairs + 1)),
            pltpu.SemaphoreType.DMA((W,)),
            pltpu.SemaphoreType.DMA((W,)),
            pltpu.SemaphoreType.DMA((W,)),
            pltpu.SemaphoreType.DMA((W,)),
        ],
        compiler_params=pltpu.CompilerParams(
            collective_id=0, has_side_effects=True, vmem_limit_bytes=60 * 1024 * 1024
        ),
    )(
        held_orders,
        pair_lows,
        state,
        inverses.reshape(2 * pairs, levels, levels),
        height,
        response,
    )


def solution(mesh):
    placed = (
        P(None, ("grp", "wave")),
        P(("grp", "wave")),
        P(("grp", "wave")),
        P(("grp", "wave"), None, None, None),
        P(),
        P(),
        P(),
        P(),
    )
    return jax.shard_map(
        shards, mesh=mesh, in_specs=placed, out_specs=P(None, ("grp", "wave")), check_vma=False
    )
```

time: 163 us -> 56.1 us (0.34)
  waiting for transfers between devices: 56.9 us -> 0 us
  Pallas kernels: 0 us -> 46.9 us
  blocking collectives: 42 us -> 0 us
  local copies, waits for them, and re-layouts: 44.3 us -> 5.61 us
  starting transfers between devices: 8.2 us -> 0 us
  matrix products: 5.05 us -> 0 us
  other arithmetic: 5.33 us -> 3.24 us
    all_to_all x2 -> x0, waiting for transfers between devices: 56.9 us -> none  [the longest x1 28.6 us: send_home(): lax.all_to_all(message, ('grp', 'wave'), split_axis=1, concat_axis=1, til...]
    pallas_call x0 -> x1, Pallas kernels: none -> 46.9 us  [shards(): pl.pallas_call(functools.partial(kernel, (Z, W, levels, slots, pairs)), o...]
    unnamed x1 -> x0, blocking collectives: 42 us -> none
    scatter x2 -> x0, local copies, waits for them, and re-layouts: 16.1 us -> none  [shards(): next_spreading_rate = jnp.zeros((layer_heights_count, fill_col), jnp.bflo...]
    gather x3 -> x0, local copies, waits for them, and re-layouts: 14.1 us -> none  [shards(): message = jnp.take(right_side, column, axis=1, mode='fill', fill_value=0)]
    all_to_all x5 -> x0, local copies, waits for them, and re-layouts: 8.52 us -> none  [the longest x4 6.22 us: send_home(): lax.all_to_all(message, ('grp', 'wave'), split_axis=1, concat_axis=1, til...]
    all_to_all x2 -> x0, starting transfers between devices: 8.2 us -> none  [the longest x1 4.4 us: send_out(): lax.all_to_all(message, ('grp', 'wave'), split_axis=1, concat_axis=1, til...]
    dot_general x4 -> x0, matrix products: 5.05 us -> none  [the longest x1 1.63 us: shards(): jnp.dot(height_operator, thermal_state_array, preferred_element_type=jnp....]
  transfers between devices with their start and end apart: 2 -> 0, of which waited for: 2 -> 0; matrix products, arithmetic and copies ran while one was open for 1% -> 0% of each run, Pallas kernels for 0% -> 0%
where the time goes in v1:
time: 56.1 us; the launch traced here: 55.8 us
  Pallas kernels  46.9 us (84%)
  local copies, waits for them, and re-layouts  5.61 us (10%)
  other arithmetic  3.24 us (6%)
    pallas_call x1, Pallas kernels, shards(): pl.pallas_call(functools.partial(kernel, (Z, W, levels, slots, pairs)), o...  46.9 us
    unnamed x2, local copies, waits for them, and re-layouts  4.21 us
    concatenate x1, other arithmetic, shards(): jnp.concatenate([jnp.zeros((levels, tail), jnp.bfloat16), height_operator...  1.62 us
    concatenate x1, other arithmetic, shards(): jnp.concatenate([through, thermal_response_matrix, mass_row[None, :]], ax...  1.53 us

profile of v1, /device:TPU:0, one launch (start us, length us, event | category | flops | bytes accessed | tf_op | source)
XLA Modules:
  0.0 55.8 jit_solution(9931072906506717801)
XLA Ops:
  0.0 0.7 %broadcast_in_dim.11 = bf16[1,137]{1,0:T(2,128)(2,1)S(1)} reshape(bf16[137]{0:T(256)(128)(2,1)} %param.15) | data formatting | bytes 548 | tf_op jit(solution)/shard_map/broadcast_in_dim | solution.py:409
  0.7 0.1 fusion.1
  0.7 0.7 %broadcast_in_dim.12 = bf16[137,1]{1,0:T(8,128)(2,1)S(1)} reshape(bf16[137]{0:T(256)(128)(2,1)} %param.13) | data formatting | bytes 548 | tf_op jit(solution)/shard_map/broadcast_in_dim | solution.py:406
  1.5 1.6 %pad_maximum_fusion.1.height = bf16[137,147]{1,0:T(8,128)(2,1)} fusion(bf16[137,1]{1,0:T(8,128)(2,1)S(1)} %broadcast_in_dim.12, bf16[137,137]{1,0:T(8,128)(2,1)} %param.12, bf16[147]{0:T(256)(128)(2,1)S(1)} %pad.3.clone), kind=kLoop, calls=%fused_computation.1 | loop fusion | flops 120834 | bytes 78384 | tf_op jit(solution)/shard_map/concatenate | solution.py:405
  3.1 1.5 %pad_maximum_fusion.response = bf16[147,137]{1,0:T(8,128)(2,1)} fusion(bf16[1,137]{1,0:T(2,128)(2,1)S(1)} %broadcast_in_dim.11, bf16[137,137]{1,0:T(8,128)(2,1)} %param.14, bf16[9,137]{1,0:T(8,128)(2,1)S(1)} %fusion.1), kind=kLoop, calls=%fused_computation | loop fusion | flops 120834 | bytes 80556 | tf_op jit(solution)/shard_map/concatenate | solution.py:409
  4.7 1.8 %copy.10 = bf16[3,2,137,137]{3,2,1,0:T(8,128)(2,1)} copy(bf16[3,2,137,137]{3,1,2,0:T(2,128)(2,1)} %param.11) | data formatting | bytes 450456 | tf_op args[3]
  6.5 46.9 %shard_map.82 = bf16[275,1930]{1,0:T(8,128)(2,1)} custom-call(s32[5]{0:T(128)} %held.1, s32[3]{0:T(128)} %lows.1, bf16[275,1930]{1,0:T(8,128)(2,1)} %state.1, bf16[6,137,137]{2,1,0:T(8,128)(2,1)} %bitcast.1, bf16[137,147]{1,0:T(8,128)(2,1)} %pad_maximum_fusion.1.height, bf16[147,137]{1,0:T(8,128)(2,1)} %pad_maximum_fusion.response), custom_call_target="tpu_custom_call" | custom-call | tf_op jit(solution)/shard_map/pallas_call | solution.py:414
  53.4 2.4 %copy.13 = bf16[275,1930]{1,0:T(8,128)(2,1)} copy(bf16[275,1930]{1,0:T(8,128)(2,1)} %shard_map.82) | data formatting | bytes 2123000
  (3 shorter events, 0.0 us)

commit v2 on v1

--- a/solution.py
+++ b/solution.py
@@ -21,11 +21,14 @@
     size,
     held,
     lows,
+    state_far,
+    inverses,
+    height_operator,
+    pressure_column,
+    thermal_response,
+    mass_row,
+    out,
     state,
-    inverses,
-    height,
-    response,
-    out,
     info,
     matrices,
     rest,
@@ -44,6 +47,7 @@
     out_recv,
     back_send,
     back_recv,
+    state_sem,
 ):
     Z, W, levels, slots, pairs = size
     half_count = Z * W * pairs
@@ -72,6 +76,8 @@
         return carry
 
     lax.fori_loop(1, devices, greet, 0)
+    fetch = pltpu.make_async_copy(state_far, state, state_sem)
+    fetch.start()
 
     lane = lax.broadcasted_iota(jnp.int32, (1, LANES), 1)
     extra = lane >= first_extra
@@ -177,7 +183,20 @@
         coefficient <= truncation - column_order, column_order + coefficient, coefficient - 1
     )
     lap_scale = (degree * (degree + 1)).astype(jnp.float32) / denom
-    drive = jnp.dot(height[...], state[LANES:, :], preferred_element_type=jnp.float32)
+    height = height_operator[...].astype(jnp.float32)
+    pressure_row = jnp.broadcast_to(
+        pressure_column[...].astype(jnp.float32).reshape(1, levels), height.shape
+    )
+    across = lax.broadcasted_iota(jnp.int32, height.shape, 1)
+    down = lax.broadcasted_iota(jnp.int32, height.shape, 0)
+    pressure_side = jnp.sum(
+        jnp.where(across == down, pressure_row, 0.0), axis=1, keepdims=True
+    )
+    height = jnp.concatenate(
+        [jnp.zeros((levels, tail), jnp.float32), height, pressure_side], axis=1
+    ).astype(jnp.bfloat16)
+    fetch.wait()
+    drive = jnp.dot(height, state[LANES:, :], preferred_element_type=jnp.float32)
     right[0:levels, :] = (
         state[0:levels, :].astype(jnp.float32) + lap_scale * drive
     ).astype(jnp.bfloat16)
@@ -245,13 +264,10 @@
         out_copy(k).start()
         return carry
 
-    middle = W // 2 + 1
-    lax.fori_loop(1, middle, send, 0)
-    relay(1)
-    lax.fori_loop(middle, W, send, 0)
+    lax.fori_loop(1, W, send, 0)
     arrived[0] = message(0)
 
-    for t in range(2, Z - 1):
+    for t in range(1, Z - 1):
         relay(t)
 
     def wait_out(k, carry):
@@ -334,6 +350,16 @@
         solve(t)
 
     total[...] = jnp.zeros_like(total)
+    through_row = lax.broadcasted_iota(jnp.int32, (tail, levels), 0)
+    through_lane = lax.broadcasted_iota(jnp.int32, (tail, levels), 1)
+    response = jnp.concatenate(
+        [
+            jnp.where(through_lane == through_row + LANES, -1.0, 0.0),
+            thermal_response[...].astype(jnp.float32),
+            mass_row[...].astype(jnp.float32).reshape(1, levels),
+        ],
+        axis=0,
+    ).astype(jnp.bfloat16)
 
     def collect(k, block):
         if not keep:
@@ -352,7 +378,7 @@
     lax.fori_loop(1, W, gather_back, 0)
 
     div = total[0:levels, :].astype(jnp.bfloat16)
-    change = jnp.dot(response[...], div, preferred_element_type=jnp.float32)
+    change = jnp.dot(response, div, preferred_element_type=jnp.float32)
     old = state[LANES:, :].astype(jnp.float32)
     below = lax.broadcasted_iota(jnp.int32, old.shape, 0) < tail
     new = jnp.where(below, 0.0, old) - change
@@ -400,13 +426,7 @@
     Z, W = lax.axis_size("grp"), lax.axis_size("wave")
     devices = Z * W
     width = state.shape[1]
-    tail = levels - LANES
     rows = ceil_to(levels, ROWS_TILE)
-    height = jnp.concatenate(
-        [jnp.zeros((levels, tail), jnp.bfloat16), height_operator, pressure_column[:, None]], axis=1
-    )
-    through = -jnp.eye(tail, levels, LANES, dtype=jnp.bfloat16)
-    response = jnp.concatenate([through, thermal_response_matrix, mass_row[None, :]], axis=0)
     places = W if W * width * 4 * LANES <= KEEP_BYTES else 1
     vmem = pl.BlockSpec(memory_space=pltpu.VMEM)
     smem = pl.BlockSpec(memory_space=pltpu.SMEM)
@@ -414,9 +434,10 @@
     return pl.pallas_call(
         functools.partial(kernel, (Z, W, levels, slots, pairs)),
         out_shape=jax.ShapeDtypeStruct(state.shape, jnp.bfloat16),
-        in_specs=[smem, smem, vmem, vmem, vmem, vmem],
+        in_specs=[smem, smem, pl.BlockSpec(memory_space=pl.ANY)] + [vmem] * 5,
         out_specs=vmem,
         scratch_shapes=[
+            pltpu.VMEM(state.shape, jnp.bfloat16),
             pltpu.VMEM((devices, pairs + 1, LANES), jnp.int32),
             pltpu.VMEM((Z, 2 * pairs, rows, levels), jnp.bfloat16),
             pltpu.VMEM((Z, rows, LANES), jnp.bfloat16),
@@ -435,6 +456,7 @@
             pltpu.SemaphoreType.DMA((W,)),
             pltpu.SemaphoreType.DMA((W,)),
             pltpu.SemaphoreType.DMA((W,)),
+            pltpu.SemaphoreType.DMA,
         ],
         compiler_params=pltpu.CompilerParams(
             collective_id=0, has_side_effects=True, vmem_limit_bytes=60 * 1024 * 1024
@@ -444,8 +466,10 @@
         pair_lows,
         state,
         inverses.reshape(2 * pairs, levels, levels),
-        height,
-        response,
+        height_operator,
+        pressure_column,
+        thermal_response_matrix,
+        mass_row,
     )
 
 

time: 56.1 us -> 50.8 us (0.906)
  other arithmetic: 3.24 us -> 0 us
  local copies, waits for them, and re-layouts: 5.61 us -> 4.21 us
    concatenate x2 -> x0, other arithmetic: 3.16 us -> none  [the longest x1 1.62 us: shards(): jnp.concatenate([jnp.zeros((levels, tail), jnp.bfloat16), height_operator...]
    broadcast_in_dim x3 -> x0, local copies, waits for them, and re-layouts: 1.4 us -> none  [the longest x1 0.73 us: shards(): pressure_column[:, None]]
where the time goes in v2:
time: 50.8 us; the launch traced here: 50.6 us
  Pallas kernels  46.4 us (91%)
  local copies, waits for them, and re-layouts  4.21 us (8%)
    pallas_call x1, Pallas kernels, shards(): pl.pallas_call(functools.partial(kernel, (Z, W, levels, slots, pairs)), o...  46.4 us
    unnamed x2, local copies, waits for them, and re-layouts  4.21 us

profile of v2, /device:TPU:0, one launch (start us, length us, event | category | flops | bytes accessed | tf_op | source)
XLA Modules:
  0.0 50.6 jit_solution(1728221170699699864)
XLA Ops:
  0.0 1.8 %copy.9 = bf16[3,2,137,137]{3,2,1,0:T(8,128)(2,1)} copy(bf16[3,2,137,137]{3,1,2,0:T(2,128)(2,1)} %param.11) | data formatting | bytes 450456 | tf_op args[3]
  1.8 46.4 %shard_map.82 = bf16[275,1930]{1,0:T(8,128)(2,1)} custom-call(s32[5]{0:T(128)} %held.1, s32[3]{0:T(128)} %lows.1, bf16[275,1930]{1,0:T(8,128)(2,1)} %state_far.1, bf16[6,137,137]{2,1,0:T(8,128)(2,1)} %bitcast.1, bf16[137,137]{1,0:T(8,128)(2,1)} %height_operator.1, bf16[137]{0:T(256)(128)(2,1)} %pressure_column.1, bf16[137,137]{1,0:T(8,128)(2,1)} %thermal_response.1, ...), custom_call_target="tpu_custom_call" | custom-call | tf_op jit(solution)/shard_map/pallas_call | solution.py:434
  48.2 2.4 %copy.11 = bf16[275,1930]{1,0:T(8,128)(2,1)} copy(bf16[275,1930]{1,0:T(8,128)(2,1)} %shard_map.82) | data formatting | bytes 2123000
